TPU v7x, 32 devices: a whole 2x2x4 slice. The times are simulated.
32 devices in a mesh: seq: 8 (over z, x), head: 2 (over y), dp: 2 (over core).
Axes of the slice: x: 2, y: 2, z: 4, core: 2. Of those that a mesh axis runs over, the one named last changes fastest.
Arguments:
- queries: bfloat16 [8192, 4096], P(('dp', 'seq'), 'head'), parts along dimension 0, may hold values from -200 to 200
- keys: bfloat16 [8192, 1024], P(('dp', 'seq'), 'head'), parts along dimension 0, may hold values from -4 to 4
- values: bfloat16 [8192, 1024], P(('dp', 'seq'), 'head'), parts along dimension 0, may hold values from -15 to 15
- doc_ids: int32 [8192], P(('dp', 'seq')), parts along dimension 0, may hold values from 0 to 7, as said below
- block_lists: int32 [64, 16], P(('dp', 'seq')), parts along dimension 0, may hold values from 0 to 32, as said below
- w_out: bfloat16 [4096, 4096], P('head'), may hold values from -0.09375 to 0.09375
Outputs:
- mixed: bfloat16 [8192, 4096], P(('dp', 'seq'), 'head'), parts along dimension 0
There are 2 independent parts, one for each index of `dp`. A program takes and returns all parts, laid end to end along the dimension named above; an argument that names none is the same for every part. Nothing has to cross between parts.
Inputs may be any that keep to these rules, and one draw needn't show every extreme that they name: `block_lists`: row i lists the blocks that query block i reads: 16 entries, each a block of the sequence or the null value 32; the non-null entries of a row are distinct and include i. Blocks k * 4 to k * 4 + 3 lie on index k of seq; over the rows of one index of seq together, at most one distinct block of each other index of seq is named (so each index of seq sends at most one of its blocks to each other index). `doc_ids`: never falling along the sequence.
All inputs are finite; a program needn't handle non-finite values.
Results may differ from a plain program's by a relative error of at most 0.013.
Values may be sent and summed in bfloat16 or wider, within the bound.
A program may use at most 128 MiB of HBM per device.

v0:
```python
import math

import jax
import jax.numpy as jnp
from jax import lax
from jax.sharding import PartitionSpec as P

QUERY_HEADS = 32
KEY_VALUE_HEADS = 8
HEAD_SIZE = 128
BLOCK_TOKENS = 128
DOCS = 8


negative = -1e30
far_position = 1073741824


def block_terms(query_block, key_rows, value_rows, allowed):
    scores = jnp.einsum(
        "qhge,jkhe->hgqjk", query_block, key_rows, preferred_element_type=jnp.float32
    ) * (1.0 / math.sqrt(HEAD_SIZE))
    masked = jnp.where(allowed[None, None], scores, negative)
    block_top = jnp.max(masked, axis=-1)
    probs = jnp.where(allowed[None, None], jnp.exp(masked - block_top[..., None]), 0.0)
    block_sum = jnp.sum(probs, axis=-1)
    weights = probs.astype(jnp.bfloat16)
    partial_value = jnp.einsum(
        "hgqjk,jkhe->hgqje", weights, value_rows, preferred_element_type=jnp.float32
    )
    return (block_top, block_sum, partial_value)


def finish(block_top, block_sum, partial_value):
    row_peak = jnp.max(block_top, axis=-1)
    factor = jnp.exp(block_top - row_peak[..., None])
    numer = jnp.sum(factor[..., None] * partial_value, axis=3)
    denom = jnp.sum(factor * block_sum, axis=-1)
    result = numer / denom[..., None]
    rows = result.shape[2]
    return jnp.transpose(result, (2, 0, 1, 3)).reshape(rows, -1).astype(jnp.bfloat16)


def per_device(queries, keys, values, doc_ids, block_lists, w_out):
    tok_rows = queries.shape[0]
    blocks_dev = tok_rows // BLOCK_TOKENS
    key_width = keys.shape[1]
    kv_heads = key_width // HEAD_SIZE
    group_count = QUERY_HEADS // KEY_VALUE_HEADS
    seq_count = lax.axis_size("seq")
    own_index = lax.axis_index("seq")
    block_count = blocks_dev * seq_count
    positions = own_index * tok_rows + jnp.arange(tok_rows, dtype=jnp.int32)
    doc_range = jnp.arange(DOCS, dtype=jnp.int32)
    doc_match = doc_ids[:, None] == doc_range[None, :]
    first_local = jnp.min(jnp.where(doc_match, positions[:, None], far_position), axis=0)
    firsts = lax.pmin(first_local, "seq")
    later = doc_range[None, :] > doc_range[:, None]
    ends_doc = jnp.min(jnp.where(later, firsts[None, :], far_position), axis=1)
    starts = jnp.sum(jnp.where(doc_match, firsts[None, :], 0), axis=1)
    ends = jnp.sum(jnp.where(doc_match, ends_doc[None, :], 0), axis=1)
    query_tiles = queries.reshape(blocks_dev, BLOCK_TOKENS, kv_heads, group_count, HEAD_SIZE)
    starts_blk = starts.reshape(blocks_dev, BLOCK_TOKENS)
    ends_blk = ends.reshape(blocks_dev, BLOCK_TOKENS)
    kv_local = jnp.concatenate([keys, values], axis=1)
    kv_blocks = kv_local.reshape(blocks_dev, BLOCK_TOKENS, 2 * key_width)
    inside = jnp.arange(BLOCK_TOKENS, dtype=jnp.int32)

    def split_rows(slot_rows):
        slots = slot_rows.shape[0]
        key_part = slot_rows[..., :key_width].reshape(slots, BLOCK_TOKENS, kv_heads, HEAD_SIZE)
        value_part = slot_rows[..., key_width:].reshape(slots, BLOCK_TOKENS, kv_heads, HEAD_SIZE)
        return (key_part, value_part)

    def allowed_mask(block_ids, usable, query_start, query_end):
        key_pos = block_ids[:, None] * BLOCK_TOKENS + inside[None, :]
        return (
            usable[None, :, None]
            & (key_pos[None] < query_end[:, None, None])
            & (key_pos[None] >= query_start[:, None, None])
        )

    valid_slot = block_lists < block_count
    owner_dev = block_lists // blocks_dev
    offset = block_lists % blocks_dev
    local_slot = owner_dev == own_index
    peer_ids = jnp.arange(seq_count, dtype=jnp.int32)
    wanted = (owner_dev[..., None] == peer_ids) & valid_slot[..., None] & (peer_ids != own_index)
    want_any = jnp.any(wanted, axis=(0, 1))
    want_offset = jnp.max(jnp.where(wanted, offset[..., None], 0), axis=(0, 1))
    request = jnp.stack([want_offset, want_any.astype(jnp.int32)], axis=1)
    granted = lax.all_to_all(request, "seq", split_axis=0, concat_axis=0, tiled=True)
    send_offset = granted[:, 0]
    send_any = granted[:, 1] > 0
    picker = (
        (send_offset[:, None] == jnp.arange(blocks_dev, dtype=jnp.int32)[None, :])
        & send_any[:, None]
    ).astype(jnp.bfloat16)
    outgoing = jnp.einsum(
        "rb,bkc->rkc", picker, kv_blocks, preferred_element_type=jnp.float32
    ).astype(jnp.bfloat16)
    arrived = lax.all_to_all(outgoing, "seq", split_axis=0, concat_axis=0, tiled=True)
    table = jnp.concatenate([kv_blocks, arrived], axis=0)

    def after_step(inputs):
        (
            query_block,
            lists_row,
            valid_row,
            owner_row,
            offset_row,
            local_row,
            query_start,
            query_end,
        ) = inputs
        slot_index = jnp.where(local_row, offset_row, blocks_dev + owner_row)
        slot_index = jnp.where(valid_row, slot_index, 0)
        key_part, value_part = split_rows(jnp.take(table, slot_index, axis=0))
        allowed = allowed_mask(lists_row, valid_row, query_start, query_end)
        return finish(*block_terms(query_block, key_part, value_part, allowed))

    attn = lax.map(
        after_step,
        (query_tiles, block_lists, valid_slot, owner_dev, offset, local_slot, starts_blk, ends_blk),
    )
    attn = attn.reshape(tok_rows, -1)
    projected = jnp.dot(attn, w_out, preferred_element_type=jnp.float32).astype(jnp.bfloat16)
    summed = lax.psum_scatter(projected, "head", scatter_dimension=1, tiled=True).astype(
        jnp.float32
    )
    return summed.astype(jnp.bfloat16)


def solution(mesh):
    in_specs = (
        P(("dp", "seq"), "head"),
        P(("dp", "seq"), "head"),
        P(("dp", "seq"), "head"),
        P(("dp", "seq")),
        P(("dp", "seq"), None),
        P("head", None),
    )
    out_specs = P(("dp", "seq"), "head")
    return jax.shard_map(
        per_device, mesh=mesh, in_specs=in_specs, out_specs=out_specs, check_vma=False
    )
```

profile of v0, /device:TPU:0, one launch (start us, length us, event | category | flops | bytes accessed | tf_op | source)
XLA Modules:
  0.0 331.9 jit_solution(6861483093592396369)
XLA Ops:
  6.5 1.3 broadcast_compare_fusion
  7.8 1.3 add_select_fusion
  10.8 7.3 %all-to-all-start = ((s32[8,1,2]{2,1,0:T(1,128)}), s32[8,1,2]{2,1,0:T(1,128)S(1)}, u32[]{:S(2)}, u32[]{:S(2)}) async-start(s32[8,1,2]{2,1,0:T(1,128)} %copy.51), calls=%async_computation | async-start | bytes 8192 | tf_op jit(solution)/shard_map/all_to_all | solution.py:92
  18.1 1.3 pad_maximum_fusion.1
  19.5 5.1 %all-to-all-done = s32[8,1,2]{2,1,0:T(1,128)S(1)} async-done(((s32[8,1,2]{2,1,0:T(1,128)}), s32[8,1,2]{2,1,0:T(1,128)S(1)}, u32[]{:S(2)}, u32[]{:S(2)}) %all-to-all-start) | async-done | bytes 96 | tf_op jit(solution)/shard_map/all_to_all | solution.py:92
  24.6 1.1 convolution_convert_fusion.1
  25.8 2.4 copy.54
  28.2 4.3 %all-to-all-start.1 = ((bf16[8,128,1024]{2,1,0:T(8,128)(2,1)}), bf16[8,128,1024]{2,1,0:T(8,128)(2,1)}, u32[]{:S(2)}, u32[]{:S(2)}) async-start(bf16[8,128,1024]{2,1,0:T(8,128)(2,1)} %copy.54), calls=%async_computation.1 | async-start | bytes 4194304 | tf_op jit(solution)/shard_map/all_to_all | solution.py:102
  32.8 47.0 %pmin.7 = s32[8]{0:T(128)S(1)} all-reduce(s32[8]{0:T(128)S(1)} %select_reduce_fusion.3), channel_id=1, replica_groups=mesh['seq'=8,'head'=2,'dp'=2] {'seq'}, use_global_device_ids=true, to_apply=%region_1.2 | all-reduce | flops 8 | bytes 64 | tf_op jit(solution)/shard_map/pmin | solution.py:57
  79.8 2.7 reshape.182
  83.4 2.1 pad_maximum_fusion
  85.5 171.5 %while.11 = (s32[]{:T(128)}, bf16[4,128,2048]{2,1,0:T(8,128)(2,1)}, pred[4,16]{1,0:T(4,128)(4,1)S(1)}, s32[4,16]{1,0:T(4,128)}, s32[4,128]{1,0:T(4,128)}, /*inde...) while((s32[]{:T(128)}, bf16[4,128,2048]{2,1,0:T(8,128)(2,1)}, ...), condition=%wide.region_13.14_spmd.clone, body=%wide.region_7.13_spmd.clone.sunk | while | flops 2218032384 | bytes 197190128 | solution.py:122
  88.2 2.7 gather_fusion
  91.0 2.6 broadcast_select_fusion.2
  93.6 2.6 fusion.58
  96.2 3.0 copy.89
  99.3 1.2 constant_dynamic-slice_fusion.9
  100.5 3.1 fusion.59
  103.6 5.3 %fusion.60 = (f32[4,4,128,16]{2,1,3,0:T(4,128)S(1)}, f32[4,4,128]{2,1,0:T(4,128)S(1)}) fusion(f32[4,16,128,128,4]{3,2,4,1,0:T(8,128)S(1)} %get-tuple-element.284, f32[4,4,128,16]{2,1,3,0:T(4,128)S(1)} %get-tuple-element.285, pred[128,16,128]{0,2,1:T(8,128)(4,1)S(1)} %compare_and_fusion.5), kind=kLoop, calls=%fused_computation.6.clone.1 | loop fusion | flops 25131008 | bytes 17309696 | tf_op jit(solution)/shard_map/while/body/eval_jaxpr/reduce_sum | solution.py:26
  108.9 1.0 copy-done
  110.6 2.4 copy.90
  113.0 10.5 %fusion.61 = f32[4,4,128,128]{2,3,1,0:T(8,128)S(1)} fusion(f32[4,16,128,128,4]{3,2,4,1,0:T(8,128)} %copy-done, f32[4,4,128,16]{2,1,3,0:T(4,128)S(1)} %get-tuple-element.285, f32[4,4,128,16]{2,1,3,0:T(4,128)} %get-tuple-element.288, pred[128,16,128]{0,2,1:T(8,128)(4,1)S(1)} %compare_and_fusion.5, bf16[16,128,4,128,1]{1,3,2,0,4:T(8,128)(2,1)} %bitcast.103), kind=kOutput, calls=%fused_computation.3.clone.1 | convolution fusion | flops 1102839808 | bytes 20447232 | tf_op jit(solution)/shard_map/while/body/eval_jaxpr/hgqjk,jkhe->hgqje/dot_general | solution.py:28
  123.6 0.9 fusion.62
  124.5 2.1 copy.91
  126.5 1.9 constant_dynamic-update-slice_fusion.2
  131.1 2.7 gather_fusion
  133.8 2.6 broadcast_select_fusion.2
  136.5 2.6 fusion.58
  139.1 3.0 copy.89
  142.1 1.2 constant_dynamic-slice_fusion.9
  143.4 3.1 fusion.59
  146.5 5.3 %fusion.60 = (f32[4,4,128,16]{2,1,3,0:T(4,128)S(1)}, f32[4,4,128]{2,1,0:T(4,128)S(1)}) fusion(f32[4,16,128,128,4]{3,2,4,1,0:T(8,128)S(1)} %get-tuple-element.284, f32[4,4,128,16]{2,1,3,0:T(4,128)S(1)} %get-tuple-element.285, pred[128,16,128]{0,2,1:T(8,128)(4,1)S(1)} %compare_and_fusion.5), kind=kLoop, calls=%fused_computation.6.clone.1 | loop fusion | flops 25131008 | bytes 17309696 | tf_op jit(solution)/shard_map/while/body/eval_jaxpr/reduce_sum | solution.py:26
  151.7 1.0 copy-done
  153.5 2.4 copy.90
  155.9 10.5 %fusion.61 = f32[4,4,128,128]{2,3,1,0:T(8,128)S(1)} fusion(f32[4,16,128,128,4]{3,2,4,1,0:T(8,128)} %copy-done, f32[4,4,128,16]{2,1,3,0:T(4,128)S(1)} %get-tuple-element.285, f32[4,4,128,16]{2,1,3,0:T(4,128)} %get-tuple-element.288, pred[128,16,128]{0,2,1:T(8,128)(4,1)S(1)} %compare_and_fusion.5, bf16[16,128,4,128,1]{1,3,2,0,4:T(8,128)(2,1)} %bitcast.103), kind=kOutput, calls=%fused_computation.3.clone.1 | convolution fusion | flops 1102839808 | bytes 20447232 | tf_op jit(solution)/shard_map/while/body/eval_jaxpr/hgqjk,jkhe->hgqje/dot_general | solution.py:28
  166.4 0.9 fusion.62
  167.3 2.1 copy.91
  169.4 1.9 constant_dynamic-update-slice_fusion.2
  174.0 2.7 gather_fusion
  176.7 2.6 broadcast_select_fusion.2
  179.4 2.6 fusion.58
  182.0 3.0 copy.89
  185.0 1.2 constant_dynamic-slice_fusion.9
  186.2 3.1 fusion.59
  189.3 5.3 %fusion.60 = (f32[4,4,128,16]{2,1,3,0:T(4,128)S(1)}, f32[4,4,128]{2,1,0:T(4,128)S(1)}) fusion(f32[4,16,128,128,4]{3,2,4,1,0:T(8,128)S(1)} %get-tuple-element.284, f32[4,4,128,16]{2,1,3,0:T(4,128)S(1)} %get-tuple-element.285, pred[128,16,128]{0,2,1:T(8,128)(4,1)S(1)} %compare_and_fusion.5), kind=kLoop, calls=%fused_computation.6.clone.1 | loop fusion | flops 25131008 | bytes 17309696 | tf_op jit(solution)/shard_map/while/body/eval_jaxpr/reduce_sum | solution.py:26
  194.6 1.0 copy-done
  196.3 2.4 copy.90
  198.8 10.5 %fusion.61 = f32[4,4,128,128]{2,3,1,0:T(8,128)S(1)} fusion(f32[4,16,128,128,4]{3,2,4,1,0:T(8,128)} %copy-done, f32[4,4,128,16]{2,1,3,0:T(4,128)S(1)} %get-tuple-element.285, f32[4,4,128,16]{2,1,3,0:T(4,128)} %get-tuple-element.288, pred[128,16,128]{0,2,1:T(8,128)(4,1)S(1)} %compare_and_fusion.5, bf16[16,128,4,128,1]{1,3,2,0,4:T(8,128)(2,1)} %bitcast.103), kind=kOutput, calls=%fused_computation.3.clone.1 | convolution fusion | flops 1102839808 | bytes 20447232 | tf_op jit(solution)/shard_map/while/body/eval_jaxpr/hgqjk,jkhe->hgqje/dot_general | solution.py:28
  210.2 2.1 copy.91
  212.3 1.9 constant_dynamic-update-slice_fusion.2
  216.8 2.7 gather_fusion
  219.6 2.6 broadcast_select_fusion.2
  222.2 2.6 fusion.58
  224.8 3.0 copy.89
  227.9 1.2 constant_dynamic-slice_fusion.9
  229.1 3.1 fusion.59
  232.2 5.3 %fusion.60 = (f32[4,4,128,16]{2,1,3,0:T(4,128)S(1)}, f32[4,4,128]{2,1,0:T(4,128)S(1)}) fusion(f32[4,16,128,128,4]{3,2,4,1,0:T(8,128)S(1)} %get-tuple-element.284, f32[4,4,128,16]{2,1,3,0:T(4,128)S(1)} %get-tuple-element.285, pred[128,16,128]{0,2,1:T(8,128)(4,1)S(1)} %compare_and_fusion.5), kind=kLoop, calls=%fused_computation.6.clone.1 | loop fusion | flops 25131008 | bytes 17309696 | tf_op jit(solution)/shard_map/while/body/eval_jaxpr/reduce_sum | solution.py:26
  237.5 1.0 copy-done
  239.2 2.4 copy.90
  241.6 10.5 %fusion.61 = f32[4,4,128,128]{2,3,1,0:T(8,128)S(1)} fusion(f32[4,16,128,128,4]{3,2,4,1,0:T(8,128)} %copy-done, f32[4,4,128,16]{2,1,3,0:T(4,128)S(1)} %get-tuple-element.285, f32[4,4,128,16]{2,1,3,0:T(4,128)} %get-tuple-element.288, pred[128,16,128]{0,2,1:T(8,128)(4,1)S(1)} %compare_and_fusion.5, bf16[16,128,4,128,1]{1,3,2,0,4:T(8,128)(2,1)} %bitcast.103), kind=kOutput, calls=%fused_computation.3.clone.1 | convolution fusion | flops 1102839808 | bytes 20447232 | tf_op jit(solution)/shard_map/while/body/eval_jaxpr/hgqjk,jkhe->hgqje/dot_general | solution.py:28
  253.1 2.1 copy.91
  255.1 1.9 constant_dynamic-update-slice_fusion.2
  257.0 14.3 %convolution_convert_fusion = bf16[512,4096]{1,0:T(8,128)(2,1)} fusion(bf16[512,2048]{1,0:T(8,128)(2,1)} %bitcast.110, bf16[2048,4096]{1,0:T(8,128)(2,1)} %param.13), kind=kOutput, calls=%fused_computation.51 | convolution fusion | flops 8592031744 | bytes 23068672 | tf_op jit(solution)/shard_map/dot_general | solution.py:127
  271.4 53.6 %reduce-scatter.2.cloned.1.call-done = bf16[512,2048]{1,0:T(8,128)(2,1)} async-done(((bf16[512,4096]{1,0:T(8,128)(2,1)}), bf16[512,2048]{1,0:T(8,128)(2,1)}) %reduce-scatter.2.cloned.1.call-update) | async-done | bytes 2097168 | tf_op jit(solution)/shard_map/reduce_scatter | solution.py:128
  (85 shorter events, 18.2 us)
Async XLA Ops:
  10.8 13.7 %all-to-all-start = ((s32[8,1,2]{2,1,0:T(1,128)}), s32[8,1,2]{2,1,0:T(1,128)S(1)}, u32[]{:S(2)}, u32[]{:S(2)}) async-start(s32[8,1,2]{2,1,0:T(1,128)} %copy.51), calls=%async_computation | async-start | bytes 8192 | tf_op jit(solution)/shard_map/all_to_all | solution.py:92
  19.4 8.8 %copy-start.4 = (bf16[512,1024]{1,0:T(8,128)(2,1)}, bf16[512,1024]{1,0:T(8,128)(2,1)S(1)}, u32[]{:S(2)}) copy-start(bf16[512,1024]{1,0:T(8,128)(2,1)S(1)} %pad_maximum_fusion.1) | copy-start | bytes 3145732
  25.8 6.9 %copy-start.6 = (s32[512]{0:T(512)S(1)}, s32[512]{0:T(512)}, u32[]{:S(2)}) copy-start(s32[512]{0:T(512)} %param.11) | copy-start | bytes 6148
  25.8 54.0 %copy-start.5 = (bf16[512,2048]{1,0:T(8,128)(2,1)S(1)}, bf16[512,2048]{1,0:T(8,128)(2,1)}, u32[]{:S(2)}) copy-start(bf16[512,2048]{1,0:T(8,128)(2,1)} %param.8) | copy-start | bytes 6291460
  28.2 55.1 %all-to-all-start.1 = ((bf16[8,128,1024]{2,1,0:T(8,128)(2,1)}), bf16[8,128,1024]{2,1,0:T(8,128)(2,1)}, u32[]{:S(2)}, u32[]{:S(2)}) async-start(bf16[8,128,1024]{2,1,0:T(8,128)(2,1)} %copy.54), calls=%async_computation.1 | async-start | bytes 4194304 | tf_op jit(solution)/shard_map/all_to_all | solution.py:102
  32.6 292.4 %reduce-scatter.2.cloned.1.call-start = ((), (), s32[]{:S(2)}) async-start(), calls=%async_computation.3 | async-start | bytes 6291456 | tf_op jit(solution)/shard_map/reduce_scatter | solution.py:128
  85.5 5.5 %copy-start.2 = (bf16[12,128,1024]{2,1,0:T(8,128)(2,1)}, bf16[12,128,1024]{2,1,0:T(8,128)(2,1)S(1)}, u32[]{:S(2)}) copy-start(bf16[12,128,1024]{2,1,0:T(8,128)(2,1)S(1)} %get-tuple-element.324) | copy-start | bytes 9437188 | tf_op jit(solution)/shard_map/while
  103.6 6.3 %copy-start = (f32[4,16,128,128,4]{3,2,4,1,0:T(8,128)}, f32[4,16,128,128,4]{3,2,4,1,0:T(8,128)S(1)}, u32[]{:S(2)}) copy-start(f32[4,16,128,128,4]{3,2,4,1,0:T(8,128)S(1)} %get-tuple-element.284) | copy-start | bytes 50331652 | tf_op jit(solution)/shard_map/while
  103.6 7.0 %copy-start.1 = (bf16[16,128,512]{2,1,0:T(8,128)(2,1)S(1)}, bf16[16,128,512]{2,1,0:T(8,128)(2,1)}, u32[]{:S(2)}) copy-start(bf16[16,128,512]{2,1,0:T(8,128)(2,1)} %get-tuple-element.289) | copy-start | bytes 6291460 | tf_op jit(solution)/shard_map/while
  113.0 15.4 %copy-start.3 = (bf16[12,128,1024]{2,1,0:T(8,128)(2,1)S(1)}, bf16[12,128,1024]{2,1,0:T(8,128)(2,1)}, u32[]{:S(2)}) copy-start(bf16[12,128,1024]{2,1,0:T(8,128)(2,1)} %copy-done.2) | copy-start | bytes 9437188 | tf_op jit(solution)/shard_map/while
  128.4 5.4 %copy-start.2 = (bf16[12,128,1024]{2,1,0:T(8,128)(2,1)}, bf16[12,128,1024]{2,1,0:T(8,128)(2,1)S(1)}, u32[]{:S(2)}) copy-start(bf16[12,128,1024]{2,1,0:T(8,128)(2,1)S(1)} %get-tuple-element.324) | copy-start | bytes 9437188 | tf_op jit(solution)/shard_map/while
  146.5 6.3 %copy-start = (f32[4,16,128,128,4]{3,2,4,1,0:T(8,128)}, f32[4,16,128,128,4]{3,2,4,1,0:T(8,128)S(1)}, u32[]{:S(2)}) copy-start(f32[4,16,128,128,4]{3,2,4,1,0:T(8,128)S(1)} %get-tuple-element.284) | copy-start | bytes 50331652 | tf_op jit(solution)/shard_map/while
  146.5 7.0 %copy-start.1 = (bf16[16,128,512]{2,1,0:T(8,128)(2,1)S(1)}, bf16[16,128,512]{2,1,0:T(8,128)(2,1)}, u32[]{:S(2)}) copy-start(bf16[16,128,512]{2,1,0:T(8,128)(2,1)} %get-tuple-element.289) | copy-start | bytes 6291460 | tf_op jit(solution)/shard_map/while
  155.9 15.4 %copy-start.3 = (bf16[12,128,1024]{2,1,0:T(8,128)(2,1)S(1)}, bf16[12,128,1024]{2,1,0:T(8,128)(2,1)}, u32[]{:S(2)}) copy-start(bf16[12,128,1024]{2,1,0:T(8,128)(2,1)} %copy-done.2) | copy-start | bytes 9437188 | tf_op jit(solution)/shard_map/while
  171.3 5.4 %copy-start.2 = (bf16[12,128,1024]{2,1,0:T(8,128)(2,1)}, bf16[12,128,1024]{2,1,0:T(8,128)(2,1)S(1)}, u32[]{:S(2)}) copy-start(bf16[12,128,1024]{2,1,0:T(8,128)(2,1)S(1)} %get-tuple-element.324) | copy-start | bytes 9437188 | tf_op jit(solution)/shard_map/while
  189.3 6.3 %copy-start = (f32[4,16,128,128,4]{3,2,4,1,0:T(8,128)}, f32[4,16,128,128,4]{3,2,4,1,0:T(8,128)S(1)}, u32[]{:S(2)}) copy-start(f32[4,16,128,128,4]{3,2,4,1,0:T(8,128)S(1)} %get-tuple-element.284) | copy-start | bytes 50331652 | tf_op jit(solution)/shard_map/while
  189.3 7.0 %copy-start.1 = (bf16[16,128,512]{2,1,0:T(8,128)(2,1)S(1)}, bf16[16,128,512]{2,1,0:T(8,128)(2,1)}, u32[]{:S(2)}) copy-start(bf16[16,128,512]{2,1,0:T(8,128)(2,1)} %get-tuple-element.289) | copy-start | bytes 6291460 | tf_op jit(solution)/shard_map/while
  198.8 15.4 %copy-start.3 = (bf16[12,128,1024]{2,1,0:T(8,128)(2,1)S(1)}, bf16[12,128,1024]{2,1,0:T(8,128)(2,1)}, u32[]{:S(2)}) copy-start(bf16[12,128,1024]{2,1,0:T(8,128)(2,1)} %copy-done.2) | copy-start | bytes 9437188 | tf_op jit(solution)/shard_map/while
  214.2 5.4 %copy-start.2 = (bf16[12,128,1024]{2,1,0:T(8,128)(2,1)}, bf16[12,128,1024]{2,1,0:T(8,128)(2,1)S(1)}, u32[]{:S(2)}) copy-start(bf16[12,128,1024]{2,1,0:T(8,128)(2,1)S(1)} %get-tuple-element.324) | copy-start | bytes 9437188 | tf_op jit(solution)/shard_map/while
  232.2 6.3 %copy-start = (f32[4,16,128,128,4]{3,2,4,1,0:T(8,128)}, f32[4,16,128,128,4]{3,2,4,1,0:T(8,128)S(1)}, u32[]{:S(2)}) copy-start(f32[4,16,128,128,4]{3,2,4,1,0:T(8,128)S(1)} %get-tuple-element.284) | copy-start | bytes 50331652 | tf_op jit(solution)/shard_map/while
  232.2 7.0 %copy-start.1 = (bf16[16,128,512]{2,1,0:T(8,128)(2,1)S(1)}, bf16[16,128,512]{2,1,0:T(8,128)(2,1)}, u32[]{:S(2)}) copy-start(bf16[16,128,512]{2,1,0:T(8,128)(2,1)} %get-tuple-element.289) | copy-start | bytes 6291460 | tf_op jit(solution)/shard_map/while
  241.6 15.4 %copy-start.3 = (bf16[12,128,1024]{2,1,0:T(8,128)(2,1)S(1)}, bf16[12,128,1024]{2,1,0:T(8,128)(2,1)}, u32[]{:S(2)}) copy-start(bf16[12,128,1024]{2,1,0:T(8,128)(2,1)} %copy-done.2) | copy-start | bytes 9437188 | tf_op jit(solution)/shard_map/while
Sparse Core Ops, SparseCore 0:
  271.5 53.4 reduce-scatter.1
where the time goes:
time: 334 us; the launch traced here: 332 us
  local copies, waits for them, and re-layouts  76.7 us (23%)
  matrix products  69.9 us (21%)
  waiting for transfers between devices  58.7 us (18%)
  other arithmetic  54 us (16%)
  blocking collectives  47 us (14%)
  between operations  13.5 us (4%)
  starting transfers between devices  11.7 us (4%)
    reduce_scatter x1, waiting for transfers between devices, per_device(): lax.psum_scatter(projected, 'head', scatter_dimension=1, tiled=True)  53.6 us
    pmin x1, blocking collectives, per_device(): firsts = lax.pmin(first_local, 'seq')  47 us
    dot_general x4, matrix products, block_terms(): jnp.einsum('hgqjk,jkhe->hgqje', weights, value_rows, preferred_element_ty...  42.1 us
    reduce_sum x4, other arithmetic, block_terms(): block_sum = jnp.sum(probs, axis=-1)  21 us
    slice x8, local copies, waits for them, and re-layouts, split_rows(): slot_rows[..., key_width:].reshape(slots, BLOCK_TOKENS, kv_heads, HEAD_SIZE)  20 us
    dynamic_update_slice x8, local copies, waits for them, and re-layouts, per_device(): lax.map(after_step, (query_tiles, block_lists, valid_slot, owner_dev, off...  15.8 us
    dot_general x1, matrix products, per_device(): jnp.dot(attn, w_out, preferred_element_type=jnp.float32)  14.3 us
    dot_general x4, matrix products, block_terms(): jnp.einsum('qhge,jkhe->hgqjk', query_block, key_rows, preferred_element_t...  12.4 us
  transfers between devices with their start and end apart: 3, of which 2 were waited for; matrix products, arithmetic and copies ran while one was open for 1% of the time, Pallas kernels for 0%

commit v1 on v0

v1 whole, which is shorter than its diff:
```python
import functools
import math

import jax
import jax.numpy as jnp
from jax import lax
from jax.experimental import pallas as pl
from jax.experimental.pallas import tpu as pltpu
from jax.sharding import PartitionSpec as P

QUERY_HEADS = 32
KEY_VALUE_HEADS = 8
HEAD_SIZE = 128
BLOCK_TOKENS = 128
DOCS = 8
GROUP = QUERY_HEADS // KEY_VALUE_HEADS
CHUNK = 4
HALVES = 2

negative = -1e30
far_position = 1073741824
exp2_scale = math.log2(math.e) / math.sqrt(HEAD_SIZE)


def attention_kernel(
    seq_count,
    blocks_dev,
    first_block,
    own_ref,
    lists_ref,
    firsts_ref,
    docs_smem,
    docs_ref,
    q_ref,
    k_ref,
    v_ref,
    rk_ref,
    rv_ref,
    out_ref,
    ktab,
    vtab,
    scores,
    acc,
    entry,
    entry_pos,
    entry_part,
    chunk_part,
    counts,
    doc_end,
    start_row,
    end_row,
):
    h = pl.program_id(0)
    i = pl.program_id(1)
    row = first_block + i
    topk = lists_ref.shape[1]
    block_count = blocks_dev * seq_count
    slots = entry.shape[1]

    @pl.when((h == 0) & (i == 0))
    def _():
        running = jnp.int32(far_position)
        for d in range(DOCS - 1, -1, -1):
            doc_end[d] = running
            running = jnp.minimum(running, firsts_ref[d])

    @pl.when(h == 0)
    def _():
        doc_first = docs_smem[row * BLOCK_TOKENS]
        doc_last = docs_smem[row * BLOCK_TOKENS + BLOCK_TOKENS - 1]
        low, low_last = firsts_ref[doc_first], firsts_ref[doc_last]
        high_first, high = doc_end[doc_first], doc_end[doc_last]
        own = own_ref[0]
        for j in range(slots):
            entry[i, j] = jnp.int32(0)
            entry_pos[i, j] = jnp.int32(far_position)
            entry_part[i, j] = jnp.int32(1)

        def add(j, count):
            block = lists_ref[row, j]
            at = block * BLOCK_TOKENS
            used = (block < block_count) & (at < high) & (at + BLOCK_TOKENS > low)
            owner = block // blocks_dev
            whole = (at >= low_last) & (at + BLOCK_TOKENS <= high_first)

            @pl.when(used)
            def _():
                entry[i, count] = jnp.where(
                    owner == own, block - owner * blocks_dev, blocks_dev + owner
                )
                entry_pos[i, count] = at
                entry_part[i, count] = jnp.where(whole, 0, 1)

            return count + jnp.where(used, 1, 0)

        count = lax.fori_loop(0, topk, add, jnp.int32(0))
        counts[i] = (count + CHUNK - 1) // CHUNK
        for c in range(slots // CHUNK):
            part = entry_part[i, c * CHUNK]
            for s in range(1, CHUNK):
                part = part + entry_part[i, c * CHUNK + s]
            chunk_part[i, c] = part
        docs = docs_ref[0]
        start = jnp.zeros((1, BLOCK_TOKENS), jnp.int32)
        end = jnp.zeros((1, BLOCK_TOKENS), jnp.int32)
        for d in range(DOCS):
            here = docs == d
            start = jnp.where(here, firsts_ref[d], start)
            end = jnp.where(here, doc_end[d], end)
        start_row[i] = jnp.broadcast_to(start, (8, BLOCK_TOKENS))
        end_row[i] = jnp.broadcast_to(end, (8, BLOCK_TOKENS))

    @pl.when(i == 0)
    def _():
        for b in range(blocks_dev):
            ktab[b] = k_ref[pl.ds(b * BLOCK_TOKENS, BLOCK_TOKENS), :]
            vtab[b] = v_ref[pl.ds(b * BLOCK_TOKENS, BLOCK_TOKENS), :]
        ktab[pl.ds(blocks_dev, seq_count)] = rk_ref[...]
        vtab[pl.ds(blocks_dev, seq_count)] = rv_ref[...]

    width = GROUP * BLOCK_TOKENS
    keys = CHUNK * BLOCK_TOKENS
    q = jnp.concatenate(
        [q_ref[:, g * HEAD_SIZE : (g + 1) * HEAD_SIZE] for g in range(GROUP)], axis=0
    )
    chunks = counts[i]

    def fold(x, op):
        return op(x.reshape(x.shape[0] // 8, 8, width), axis=0)

    def score_step(c, top):
        at = pl.multiple_of(c * keys, keys)
        k = jnp.concatenate([ktab[entry[i, c * CHUNK + s]] for s in range(CHUNK)], axis=0)
        scores[pl.ds(at, keys), :] = lax.dot_general(
            k, q, (((1,), (1,)), ((), ())), preferred_element_type=jnp.float32
        )

        @pl.when(chunk_part[i, c] > 0)
        def _():
            start = start_row[i][0:1]
            end = end_row[i][0:1]
            start = jnp.concatenate([start] * GROUP, axis=1)
            end = jnp.concatenate([end] * GROUP, axis=1)
            inside = lax.broadcasted_iota(jnp.int32, (BLOCK_TOKENS, width), 0)
            for s in range(CHUNK):
                pos = inside + entry_pos[i, c * CHUNK + s]
                here = pl.ds(at + s * BLOCK_TOKENS, BLOCK_TOKENS)
                scores[here, :] = jnp.where(
                    (pos >= start) & (pos < end), scores[here, :], negative
                )

        return jnp.maximum(top, fold(scores[pl.ds(at, keys), :], jnp.max))

    top = lax.fori_loop(0, chunks, score_step, jnp.full((8, width), negative, jnp.float32))
    top = jnp.max(top, axis=0, keepdims=True)
    acc[...] = jnp.zeros_like(acc)

    def value_step(c, total):
        at = pl.multiple_of(c * keys, keys)
        v = jnp.concatenate([vtab[entry[i, c * CHUNK + s]] for s in range(CHUNK)], axis=0)
        p = jnp.exp2((scores[pl.ds(at, keys), :] - top) * exp2_scale)
        acc[...] += lax.dot_general(
            v,
            p.astype(jnp.bfloat16),
            (((0,), (0,)), ((), ())),
            preferred_element_type=jnp.float32,
        )
        return total + fold(p, jnp.sum)

    total = lax.fori_loop(0, chunks, value_step, jnp.zeros((8, width), jnp.float32))
    total = jnp.sum(total, axis=0, keepdims=True)
    result = acc[...] / total
    for g in range(GROUP):
        out_ref[:, g * HEAD_SIZE : (g + 1) * HEAD_SIZE] = result[
            :, g * BLOCK_TOKENS : (g + 1) * BLOCK_TOKENS
        ].T.astype(jnp.bfloat16)


def attention(half, own, lists, firsts, doc_ids, queries, keys, values, arrived):
    tok_rows = queries.shape[0]
    blocks_dev = tok_rows // BLOCK_TOKENS
    kv_heads = keys.shape[1] // HEAD_SIZE
    seq_count = arrived.shape[0]
    topk = lists.shape[1]
    slots = -(-topk // CHUNK) * CHUNK
    rows = blocks_dev // HALVES
    first_block = half * rows
    width = GROUP * BLOCK_TOKENS
    smem = pl.BlockSpec(memory_space=pltpu.SMEM)
    flops = rows * kv_heads * width * 11 * BLOCK_TOKENS * HEAD_SIZE * 4
    return pl.pallas_call(
        functools.partial(attention_kernel, seq_count, blocks_dev, first_block),
        grid=(kv_heads, rows),
        out_shape=jax.ShapeDtypeStruct((rows * BLOCK_TOKENS, queries.shape[1]), jnp.bfloat16),
        in_specs=[
            smem,
            smem,
            smem,
            smem,
            pl.BlockSpec((1, 1, BLOCK_TOKENS), lambda h, i: (first_block + i, 0, 0)),
            pl.BlockSpec((BLOCK_TOKENS, width), lambda h, i: (first_block + i, h)),
            pl.BlockSpec((tok_rows, HEAD_SIZE), lambda h, i: (0, h)),
            pl.BlockSpec((tok_rows, HEAD_SIZE), lambda h, i: (0, h)),
            pl.BlockSpec((seq_count, BLOCK_TOKENS, HEAD_SIZE), lambda h, i: (0, 0, h)),
            pl.BlockSpec((seq_count, BLOCK_TOKENS, HEAD_SIZE), lambda h, i: (0, 0, kv_heads + h)),
        ],
        out_specs=pl.BlockSpec((BLOCK_TOKENS, width), lambda h, i: (i, h)),
        scratch_shapes=[
            pltpu.VMEM((blocks_dev + seq_count, BLOCK_TOKENS, HEAD_SIZE), jnp.bfloat16),
            pltpu.VMEM((blocks_dev + seq_count, BLOCK_TOKENS, HEAD_SIZE), jnp.bfloat16),
            pltpu.VMEM((slots * BLOCK_TOKENS, width), jnp.float32),
            pltpu.VMEM((HEAD_SIZE, width), jnp.float32),
            pltpu.SMEM((rows, slots), jnp.int32),
            pltpu.SMEM((rows, slots), jnp.int32),
            pltpu.SMEM((rows, slots), jnp.int32),
            pltpu.SMEM((rows, slots // CHUNK), jnp.int32),
            pltpu.SMEM((rows,), jnp.int32),
            pltpu.SMEM((DOCS,), jnp.int32),
            pltpu.VMEM((rows, 8, BLOCK_TOKENS), jnp.int32),
            pltpu.VMEM((rows, 8, BLOCK_TOKENS), jnp.int32),
        ],
        compiler_params=pltpu.CompilerParams(
            dimension_semantics=("arbitrary", "arbitrary"), vmem_limit_bytes=40 * 2**20
        ),
        cost_estimate=pl.CostEstimate(
            flops=3 * flops, bytes_accessed=8 * 2**20, transcendentals=0
        ),
    )(
        own.reshape(1),
        lists,
        firsts,
        doc_ids,
        doc_ids.reshape(blocks_dev, 1, BLOCK_TOKENS),
        queries,
        keys,
        values,
        arrived,
        arrived,
    )


def per_device(queries, keys, values, doc_ids, block_lists, w_out):
    tok_rows = queries.shape[0]
    blocks_dev = tok_rows // BLOCK_TOKENS
    key_width = keys.shape[1]
    seq_count = lax.axis_size("seq")
    head_count = lax.axis_size("head")
    own = lax.axis_index("seq")
    head = lax.axis_index("head")
    block_count = blocks_dev * seq_count
    positions = own * tok_rows + jnp.arange(tok_rows, dtype=jnp.int32)
    doc_match = doc_ids[:, None] == jnp.arange(DOCS, dtype=jnp.int32)[None, :]
    first_local = jnp.min(jnp.where(doc_match, positions[:, None], far_position), axis=0)

    owners = jnp.arange(seq_count, dtype=jnp.int32)
    wanted = (block_lists[..., None] // blocks_dev == owners) & (
        block_lists[..., None] < block_count
    )
    request = jnp.max(
        jnp.where(wanted, block_lists[..., None] % blocks_dev + 1, 0), axis=(0, 1)
    )
    notes = lax.all_gather(jnp.concatenate([first_local, request]), "seq")
    firsts = jnp.min(notes[:, :DOCS], axis=0)
    asked = lax.dynamic_index_in_dim(notes[:, DOCS:], own, 1, keepdims=False)
    kv_blocks = jnp.concatenate([keys, values], axis=1).reshape(
        blocks_dev, BLOCK_TOKENS, 2 * key_width
    )
    outgoing = kv_blocks[jnp.maximum(asked - 1, 0)]
    arrived = lax.all_to_all(outgoing, "seq", split_axis=0, concat_axis=0, tiled=True)

    cols = w_out.shape[1] // head_count
    results = []
    for half in range(HALVES):
        attn = attention(
            half, own, block_lists, firsts, doc_ids, queries, keys, values, arrived
        )
        projected = jnp.dot(attn, w_out, preferred_element_type=jnp.float32).astype(jnp.bfloat16)
        total = lax.dynamic_slice_in_dim(projected, head * cols, cols, 1).astype(jnp.float32)
        for step in range(1, head_count):
            to = lax.rem(head + step, head_count)
            part = lax.dynamic_slice_in_dim(projected, to * cols, cols, 1)
            got = lax.ppermute(
                part, "head", [(a, (a + step) % head_count) for a in range(head_count)]
            )
            total = total + got.astype(jnp.float32)
        results.append(total.astype(jnp.bfloat16))
    return jnp.concatenate(results, axis=0)


def solution(mesh):
    in_specs = (
        P(("dp", "seq"), "head"),
        P(("dp", "seq"), "head"),
        P(("dp", "seq"), "head"),
        P(("dp", "seq")),
        P(("dp", "seq"), None),
        P("head", None),
    )
    out_specs = P(("dp", "seq"), "head")
    return jax.shard_map(
        per_device, mesh=mesh, in_specs=in_specs, out_specs=out_specs, check_vma=False
    )
```

time: 334 us -> 153 us (0.46); the launches traced: 332 us -> 155 us
  local copies, waits for them, and re-layouts: 76.7 us -> 8.94 us
  matrix products: 69.9 us -> 9.79 us
  other arithmetic: 54 us -> 9.01 us
  Pallas kernels: 0 us -> 44 us
  blocking collectives: 47 us -> 13.1 us
  between operations: 13.5 us -> 0.8 us
  starting transfers between devices: 11.7 us -> 5.83 us
  waiting for transfers between devices: 58.7 us -> 63.6 us
    dot_general x9 -> x0, matrix products: 55.6 us -> none  [the longest x4 42.1 us: block_terms(): jnp.einsum('hgqjk,jkhe->hgqje', weights, value_rows, preferred_element_ty...]
    reduce_scatter x1 -> x0, waiting for transfers between devices: 53.6 us -> none  [per_device(): lax.psum_scatter(projected, 'head', scatter_dimension=1, tiled=True)]
    pmin x1 -> x0, blocking collectives: 47 us -> none  [per_device(): firsts = lax.pmin(first_local, 'seq')]
    all_to_all x1, waiting for transfers between devices: 0.01 us -> 45.7 us  [per_device(): lax.all_to_all(outgoing, 'seq', split_axis=0, concat_axis=0, tiled=True)]
    pallas_call x0 -> x2, Pallas kernels: none -> 44 us  [attention(): pl.pallas_call(functools.partial(attention_kernel, seq_count, blocks_dev,...]
    slice x12 -> x0, local copies, waits for them, and re-layouts: 32.1 us -> none  [the longest x8 20 us: split_rows(): slot_rows[..., key_width:].reshape(slots, BLOCK_TOKENS, kv_heads, HEAD_SIZE)]
    reduce_sum x9 -> x0, other arithmetic: 24.5 us -> none  [the longest x4 21 us: block_terms(): block_sum = jnp.sum(probs, axis=-1)]
    ppermute x0 -> x2, waiting for transfers between devices: none -> 17.8 us  [per_device(): lax.ppermute(part, 'head', [(a, (a + step) % head_count) for a in range(h...]
  transfers between devices with their start and end apart: 3 -> 3, of which waited for: 2 -> 2; matrix products, arithmetic and copies ran while one was open for 1% -> 4% of each run, Pallas kernels for 0% -> 14%
where the time goes in v1:
time: 153 us; the launch traced here: 155 us
  waiting for transfers between devices  63.6 us (42%)
  Pallas kernels  44 us (29%)
  blocking collectives  13.1 us (9%)
  matrix products  9.79 us (6%)
  other arithmetic  9.01 us (6%)
  local copies, waits for them, and re-layouts  8.94 us (6%)
  starting transfers between devices  5.83 us (4%)
    all_to_all x1, waiting for transfers between devices, per_device(): lax.all_to_all(outgoing, 'seq', split_axis=0, concat_axis=0, tiled=True)  45.7 us
    pallas_call x2, Pallas kernels, attention(): pl.pallas_call(functools.partial(attention_kernel, seq_count, blocks_dev,...  44 us
    ppermute x2, waiting for transfers between devices, per_device(): lax.ppermute(part, 'head', [(a, (a + step) % head_count) for a in range(h...  17.8 us
    unnamed x1, blocking collectives  13.1 us
    dot_general x2, matrix products, per_device(): jnp.dot(attn, w_out, preferred_element_type=jnp.float32)  9.79 us
    unnamed x22, local copies, waits for them, and re-layouts  5.61 us
    all_to_all x1, starting transfers between devices, per_device(): lax.all_to_all(outgoing, 'seq', split_axis=0, concat_axis=0, tiled=True)  3.75 us
    convert_element_type x2, other arithmetic, per_device(): results.append(total.astype(jnp.bfloat16))  3.25 us
  transfers between devices with their start and end apart: 3, of which 2 were waited for; matrix products, arithmetic and copies ran while one was open for 4% of the time, Pallas kernels for 14%

profile of v1, /device:TPU:0, one launch (start us, length us, event | category | flops | bytes accessed | tf_op | source)
XLA Modules:
  0.0 155.0 jit_solution(5227124983804821754)
XLA Ops:
  0.0 0.7 add_select_fusion.1
  0.7 0.7 broadcast_compare_fusion
  1.4 0.8 select_reduce_fusion.1
  2.2 1.2 dynamic-slice
  4.1 0.1 select_reduce_fusion
  4.2 0.2 add_dynamic-update-slice_fusion
  4.4 13.1 %all-reduce = s32[128]{0:T(128)S(1)} all-reduce(s32[128]{0:T(128)S(1)} %add_dynamic-update-slice_fusion), channel_id=2, replica_groups=mesh['seq'=8,'head'=2,'dp'=2] {'seq'}, use_global_device_ids=true, to_apply=%add | all-reduce | flops 128 | bytes 1024
  17.5 0.1 reshape.56
  17.5 0.1 fusion.3
  17.6 0.2 maximum_reduce_fusion
  17.8 1.4 pad_maximum_fusion.1
  19.3 2.0 %gather_fusion = bf16[8,128,1024]{2,1,0:T(8,128)(2,1)} fusion(bf16[4,128,1024]{2,1,0:T(8,128)(2,1)S(1)} %bitcast.10, s32[1024]{0:T(1024)S(1)} %pad_clamp_fusion), kind=kCustom, calls=%fused_computation | custom fusion | bytes 4194336 | tf_op jit(solution)/shard_map/gather | solution.py:268
  21.3 0.0 copy-start
  21.3 0.0 copy-start.1
  21.3 0.0 copy-start.2
  21.3 0.0 copy-start.3
  21.3 3.7 %all-to-all-start = ((bf16[8,128,1024]{2,1,0:T(8,128)(2,1)}), bf16[8,128,1024]{2,1,0:T(8,128)(2,1)S(1)}, u32[]{:S(2)}, u32[]{:S(2)}) async-start(bf16[8,128,1024]{2,1,0:T(8,128)(2,1)} %gather_fusion), calls=%async_computation | async-start | bytes 4194304 | tf_op jit(solution)/shard_map/all_to_all | solution.py:269
  25.0 45.7 %all-to-all-done.rk_ref.rv_ref = bf16[8,128,1024]{2,1,0:T(8,128)(2,1)S(1)} async-done(((bf16[8,128,1024]{2,1,0:T(8,128)(2,1)}), bf16[8,128,1024]{2,1,0:T(8,128)(2,1)S(1)}, u32[]{:S(2)}, u32[]{:S(2)}) %all-to-all-start) | async-done | bytes 2097184 | tf_op jit(solution)/shard_map/all_to_all | solution.py:269
  70.8 0.0 copy-done
  70.8 0.0 copy-done.1
  70.8 0.0 copy-done.2
  70.8 0.0 copy-done.3
  70.8 0.0 copy-start.4
  70.8 1.6 %copy-done.4 = bf16[512,2048]{1,0:T(8,128)(2,1)S(1)} copy-done((bf16[512,2048]{1,0:T(8,128)(2,1)S(1)}, bf16[512,2048]{1,0:T(8,128)(2,1)}, u32[]{:S(2)}) %copy-start.4) | copy-done | bytes 2097176
  72.4 0.0 copy-start.9
  72.4 22.0 %shard_map.64 = bf16[256,2048]{1,0:T(8,128)(2,1)S(1)} custom-call(s32[1]{0:T(128)} %bitcast.own_ref, s32[4,16]{1,0:T(4,128)S(1)} %copy-done.2, s32[8]{0:T(128)S(1)} %get-tuple-element.6.firsts_ref, s32[512]{0:T(512)S(1)} %copy-done.3, s32[4,1,128]{2,1,0:T(1,128)S(1)} %bitcast.8, bf16[512,2048]{1,0:T(8,128)(2,1)S(1)} %copy-done.4, ...), custom_call_target="tpu_custom_call" | custom-call | flops 8858370048 | bytes 8388608 | tf_op jit(solution)/shard_map/pallas_call | solution.py:191
  94.4 0.0 copy-done.9
  94.4 4.9 %convolution_convert_fusion.1 = bf16[256,4096]{1,0:T(8,128)(2,1)S(1)} fusion(bf16[256,2048]{1,0:T(8,128)(2,1)S(1)} %shard_map.64, bf16[2048,4096]{1,0:T(8,128)(2,1)S(1)} %copy-done.9), kind=kOutput, calls=%fused_computation.2 | convolution fusion | flops 4296015872 | bytes 19922944 | tf_op jit(solution)/shard_map/dot_general | solution.py:277
  99.3 0.0 copy-start.5
  99.3 1.2 constant_dynamic-slice_fusion.1
  100.5 0.5 copy-done.5
  101.0 1.5 collective-permute-start
  102.5 22.0 %shard_map.65 = bf16[256,2048]{1,0:T(8,128)(2,1)S(1)} custom-call(s32[1]{0:T(128)} %bitcast.own_ref, s32[4,16]{1,0:T(4,128)S(1)} %copy-done.2, s32[8]{0:T(128)S(1)} %get-tuple-element.6.firsts_ref, s32[512]{0:T(512)S(1)} %copy-done.3, s32[4,1,128]{2,1,0:T(1,128)S(1)} %bitcast.9, bf16[512,2048]{1,0:T(8,128)(2,1)S(1)} %copy-done.4, ...), custom_call_target="tpu_custom_call" | custom-call | flops 8858370048 | bytes 8388608 | tf_op jit(solution)/shard_map/pallas_call | solution.py:191
  124.5 4.9 %convolution_convert_fusion = bf16[256,4096]{1,0:T(8,128)(2,1)S(1)} fusion(bf16[256,2048]{1,0:T(8,128)(2,1)S(1)} %shard_map.65, bf16[2048,4096]{1,0:T(8,128)(2,1)S(1)} %copy-done.9), kind=kOutput, calls=%fused_computation.1 | convolution fusion | flops 4296015872 | bytes 19922944 | tf_op jit(solution)/shard_map/dot_general | solution.py:277
  129.4 0.0 copy-start.7
  129.4 1.3 copy-done.7
  130.7 0.0 copy-start.6
  130.7 0.1 constant_dynamic-slice_fusion
  130.8 0.6 collective-permute-start.1
  131.3 0.0 copy-start.8
  131.3 0.0 collective-permute-done
  131.3 0.9 copy-done.6
  132.3 1.6 %add_convert_fusion.1 = bf16[256,2048]{1,0:T(8,128)(2,1)S(1)} fusion(bf16[256,2048]{1,0:T(8,128)(2,1)} %collective-permute-done, bf16[256,4096]{1,0:T(8,128)(2,1)S(1)} %copy-done.6, s32[]{:T(128)S(6)} %select_n.40), kind=kLoop, calls=%fused_computation.5 | loop fusion | flops 2097152 | bytes 3145732 | tf_op jit(solution)/shard_map/convert_element_type | solution.py:286
  133.9 17.8 %collective-permute-done.1 = bf16[256,2048]{1,0:T(8,128)(2,1)} collective-permute-done((bf16[256,2048]{1,0:T(8,128)(2,1)S(1)}, bf16[256,2048]{1,0:T(8,128)(2,1)}, u32[]{:S(2)}, u32[]{:S(2)}) %collective-permute-start.1) | collective-permute-done | bytes 1048608 | tf_op jit(solution)/shard_map/ppermute | solution.py:282
  151.8 0.0 copy-done.8
  151.8 1.6 %add_convert_fusion = bf16[256,2048]{1,0:T(8,128)(2,1)S(1)} fusion(bf16[256,2048]{1,0:T(8,128)(2,1)} %collective-permute-done.1, bf16[256,4096]{1,0:T(8,128)(2,1)S(1)} %copy-done.8, s32[]{:T(128)S(6)} %select_n.40), kind=kLoop, calls=%fused_computation.4 | loop fusion | flops 2097152 | bytes 3145732 | tf_op jit(solution)/shard_map/convert_element_type | solution.py:286
  153.4 1.6 %pad_maximum_fusion = bf16[512,2048]{1,0:T(8,128)(2,1)} fusion(bf16[256,2048]{1,0:T(8,128)(2,1)S(1)} %add_convert_fusion, bf16[256,2048]{1,0:T(8,128)(2,1)S(1)} %add_convert_fusion.1), kind=kLoop, calls=%fused_computation.3 | loop fusion | flops 4194304 | bytes 4194304 | tf_op jit(solution)/shard_map/concatenate | solution.py:287
  (3 shorter events, 0.0 us)
Async XLA Ops:
  21.3 49.5 %copy-start = (bf16[512,512]{1,0:T(8,128)(2,1)S(1)}, bf16[512,512]{1,0:T(8,128)(2,1)}, u32[]{:S(2)}) copy-start(bf16[512,512]{1,0:T(8,128)(2,1)} %k_ref.3) | copy-start | bytes 1572868
  21.3 49.5 %copy-start.1 = (bf16[512,512]{1,0:T(8,128)(2,1)S(1)}, bf16[512,512]{1,0:T(8,128)(2,1)}, u32[]{:S(2)}) copy-start(bf16[512,512]{1,0:T(8,128)(2,1)} %v_ref.3) | copy-start | bytes 1572868
  21.3 49.5 %copy-start.2 = (s32[4,16]{1,0:T(4,128)S(1)}, s32[4,16]{1,0:T(4,128)}, u32[]{:S(2)}) copy-start(s32[4,16]{1,0:T(4,128)} %lists_ref.3) | copy-start | bytes 772
  21.3 49.5 %copy-start.3 = (s32[512]{0:T(512)S(1)}, s32[512]{0:T(512)}, u32[]{:S(2)}) copy-start(s32[512]{0:T(512)} %docs_smem.3) | copy-start | bytes 6148
  21.3 49.5 %all-to-all-start = ((bf16[8,128,1024]{2,1,0:T(8,128)(2,1)}), bf16[8,128,1024]{2,1,0:T(8,128)(2,1)S(1)}, u32[]{:S(2)}, u32[]{:S(2)}) async-start(bf16[8,128,1024]{2,1,0:T(8,128)(2,1)} %gather_fusion), calls=%async_computation | async-start | bytes 4194304 | tf_op jit(solution)/shard_map/all_to_all | solution.py:269
  70.8 1.6 %copy-start.4 = (bf16[512,2048]{1,0:T(8,128)(2,1)S(1)}, bf16[512,2048]{1,0:T(8,128)(2,1)}, u32[]{:S(2)}) copy-start(bf16[512,2048]{1,0:T(8,128)(2,1)} %q_ref.3) | copy-start | bytes 6291460
  72.4 22.0 %copy-start.9 = (bf16[2048,4096]{1,0:T(8,128)(2,1)S(1)}, bf16[2048,4096]{1,0:T(8,128)(2,1)}, u32[]{:S(2)}) copy-start(bf16[2048,4096]{1,0:T(8,128)(2,1)} %param.11) | copy-start | bytes 50331652
  99.3 1.7 %copy-start.5 = (bf16[256,4096]{1,0:T(8,128)(2,1)}, bf16[256,4096]{1,0:T(8,128)(2,1)S(1)}, u32[]{:S(2)}) copy-start(bf16[256,4096]{1,0:T(8,128)(2,1)S(1)} %convolution_convert_fusion.1) | copy-start | bytes 6291460
  101.0 30.4 %collective-permute-start = (bf16[256,2048]{1,0:T(8,128)(2,1)}, bf16[256,2048]{1,0:T(8,128)(2,1)}, u32[]{:S(2)}, u32[]{:S(2)}) collective-permute-start(bf16[256,2048]{1,0:T(8,128)(2,1)} %constant_dynamic-slice_fusion.1), channel_id=1, source_target_pairs={{0,2},{2,0},{1,3},{3,1},{4,6},{6,4},{5,7},{7,5},{8,10},{10,8},{9,1... | collective-permute-start | bytes 3145736 | tf_op jit(solution)/shard_map/ppermute | solution.py:282
  129.4 1.3 copy-start.7
  130.7 1.6 %copy-start.6 = (bf16[256,4096]{1,0:T(8,128)(2,1)S(1)}, bf16[256,4096]{1,0:T(8,128)(2,1)}, u32[]{:S(2)}) copy-start(bf16[256,4096]{1,0:T(8,128)(2,1)} %copy-done.5) | copy-start | bytes 6291460
  130.8 21.0 %collective-permute-start.1 = (bf16[256,2048]{1,0:T(8,128)(2,1)S(1)}, bf16[256,2048]{1,0:T(8,128)(2,1)}, u32[]{:S(2)}, u32[]{:S(2)}) collective-permute-start(bf16[256,2048]{1,0:T(8,128)(2,1)S(1)} %constant_dynamic-slice_fusion), channel_id=1, source_target_pairs={{0,2},{2,0},{1,3},{3,1},{4,6},{6,4},{5,7},{7,5},{8,10},{10,8},{9,1... | collective-permute-start | bytes 3145736 | tf_op jit(solution)/shard_map/ppermute | solution.py:282
  131.3 20.4 %copy-start.8 = (bf16[256,4096]{1,0:T(8,128)(2,1)S(1)}, bf16[256,4096]{1,0:T(8,128)(2,1)}, u32[]{:S(2)}) copy-start(bf16[256,4096]{1,0:T(8,128)(2,1)} %copy-done.7) | copy-start | bytes 6291460
